TPU v7x, 32 devices: a whole 2x2x4 slice. The times are simulated.
32 devices in a mesh: seq: 8 (over y, x, core), head: 4 (over z).
Axes of the slice: x: 2, y: 2, z: 4, core: 2. Of those that a mesh axis runs over, the one named last changes fastest.
Arguments:
- tokens: bfloat16 [32, 1024, 1024], P('seq'), may hold values from -6 to 6
- w_query: bfloat16 [1024, 1024], P(None, 'head'), may hold values from -1 to 1
- w_key: bfloat16 [1024, 1024], P(None, 'head'), may hold values from -1 to 1
- w_value: bfloat16 [1024, 1024], P(None, 'head'), may hold values from -0.1875 to 0.1875
- w_out: bfloat16 [1024, 1024], P('head'), may hold values from -0.1875 to 0.1875
Outputs:
- mixed: bfloat16 [32, 1024, 1024], P('seq', None, 'head')
All inputs are finite; a program needn't handle non-finite values.
Results may differ from a plain program's by a relative error of at most 0.012.
Values may be sent and summed in bfloat16 or wider, within the bound.
A program may use at most 128 MiB of HBM per device.

v0:
```python
import jax
import jax.numpy as jnp
from jax import lax
from jax.sharding import PartitionSpec as P

HS = 64


epsilon = 1e-05


def normalize(tokens):
    values = tokens.astype(jnp.float32)
    row_mean = jnp.mean(values, axis=-1, keepdims=True)
    centered = values - row_mean
    row_var = jnp.mean(centered * centered, axis=-1, keepdims=True)
    return (centered * lax.rsqrt(row_var + epsilon)).astype(jnp.bfloat16)


def project(source, weight):
    return jnp.einsum("fpd,dc->fpc", source, weight, preferred_element_type=jnp.float32).astype(
        jnp.bfloat16
    )


def attend(queries, key_rows, value_rows, head_count):
    frames, patch_count, feature_width = queries.shape
    head_size = feature_width // head_count
    query_flat = queries.reshape(frames, patch_count * head_count, head_size)
    key_flat = key_rows.reshape(frames, patch_count * head_count, head_size)
    value_flat = value_rows.reshape(frames, patch_count * head_count, head_size)
    scores = jnp.einsum(
        "fmd,gmd->fgm", query_flat, key_flat, preferred_element_type=jnp.float32
    ) * head_size ** (-0.5)
    row_top = jnp.max(scores, axis=1, keepdims=True)
    raised = jnp.exp(scores - row_top)
    weights = (raised / jnp.sum(raised, axis=1, keepdims=True)).astype(jnp.bfloat16)
    attended = jnp.einsum("fgm,gmd->fmd", weights, value_flat, preferred_element_type=jnp.float32)
    return attended.astype(jnp.bfloat16).reshape(frames, patch_count, feature_width)


def local(tokens, w_query, w_key, w_value, w_out):
    normed = normalize(tokens)
    head_count = w_query.shape[1] // HS
    local_query = project(normed, w_query)
    local_key = project(normed, w_key)
    local_value = project(normed, w_value)
    queries, key_rows, value_rows = (
        lax.all_to_all(local_query, "seq", split_axis=1, concat_axis=0, tiled=True),
        lax.all_to_all(local_key, "seq", split_axis=1, concat_axis=0, tiled=True),
        lax.all_to_all(local_value, "seq", split_axis=1, concat_axis=0, tiled=True),
    )
    attended = attend(queries, key_rows, value_rows, head_count)
    partial_value = jnp.einsum("fpc,cd->fpd", attended, w_out, preferred_element_type=jnp.float32)
    columns = lax.psum_scatter(
        partial_value.astype(jnp.bfloat16), "head", scatter_dimension=2, tiled=True
    )
    return lax.all_to_all(columns, "seq", split_axis=0, concat_axis=1, tiled=True)


def solution(mesh):
    return jax.shard_map(
        local,
        mesh=mesh,
        in_specs=(
            P("seq", None, None),
            P(None, "head"),
            P(None, "head"),
            P(None, "head"),
            P("head", None),
        ),
        out_specs=P("seq", None, "head"),
        check_vma=False,
    )
```

profile of v0, /device:TPU:0, one launch (start us, length us, event | category | flops | bytes accessed | tf_op | source)
XLA Modules:
  0.0 326.3 jit_solution(13314724638309537397)
XLA Ops:
  6.5 4.7 %convert_reduce_fusion = f32[4,1024]{1,0:T(4,128)S(1)} fusion(bf16[4,1024,1024]{2,1,0:T(8,128)(2,1)} %param.5), kind=kLoop, calls=%fused_computation.2 | loop fusion | flops 8384512 | bytes 8404992 | tf_op jit(solution)/shard_map/reduce_sum | solution.py:14
  11.3 1.1 copy-done.1
  12.4 2.8 fusion.3
  15.2 3.1 fusion.28
  18.4 3.0 copy.19
  21.3 5.2 %all-to-all-start.1 = ((bf16[4,1024,256]{2,0,1:T(4,128)(2,1)}), bf16[4,1024,256]{2,0,1:T(4,128)(2,1)S(1)}, u32[]{:S(2)}, u32[]{:S(2)}) async-start(bf16[4,1024,256]{2,0,1:T(4,128)(2,1)} %copy.19), calls=%async_computation.1 | async-start | bytes 4194304 | tf_op jit(solution)/shard_map/all_to_all | solution.py:50
  26.5 5.0 %fusion.31 = bf16[4,1024,256]{2,1,0:T(8,128)(2,1)S(1)} fusion(bf16[4,1024,1024]{2,1,0:T(8,128)(2,1)} %param.5, f32[4,1024]{1,0:T(4,128)S(1)} %add_rsqrt_fusion, f32[4,1024]{1,0:T(4,128)S(1)} %broadcast_multiply_fusion, bf16[1024,256]{1,0:T(8,128)(2,1)S(1)} %copy-done.4), kind=kOutput, calls=%fused_computation.30 | convolution fusion | flops 2165309440 | bytes 11042816 | tf_op jit(solution)/shard_map/fpd,dc->fpc/dot_general | solution.py:21
  31.6 2.9 copy.21
  34.5 18.6 %all-to-all-done.1 = bf16[4,1024,256]{2,0,1:T(4,128)(2,1)S(1)} async-done(((bf16[4,1024,256]{2,0,1:T(4,128)(2,1)}), bf16[4,1024,256]{2,0,1:T(4,128)(2,1)S(1)}, u32[]{:S(2)}, u32[]{:S(2)}) %all-to-all-start.1) | async-done | bytes 2097184 | tf_op jit(solution)/shard_map/all_to_all | solution.py:50
  53.1 4.3 %all-to-all-start.2 = ((bf16[4,1024,256]{2,0,1:T(4,128)(2,1)}), bf16[4,1024,256]{2,0,1:T(4,128)(2,1)}, u32[]{:S(2)}, u32[]{:S(2)}) async-start(bf16[4,1024,256]{2,0,1:T(4,128)(2,1)} %copy.21), calls=%async_computation.2 | async-start | bytes 4194304 | tf_op jit(solution)/shard_map/all_to_all | solution.py:49
  57.5 5.0 %fusion.25 = bf16[4,1024,256]{2,1,0:T(8,128)(2,1)S(1)} fusion(bf16[4,1024,1024]{2,1,0:T(8,128)(2,1)} %param.5, f32[4,1024]{1,0:T(4,128)S(1)} %add_rsqrt_fusion, f32[4,1024]{1,0:T(4,128)S(1)} %broadcast_multiply_fusion, bf16[1024,256]{1,0:T(8,128)(2,1)S(1)} %copy-done.5), kind=kOutput, calls=%fused_computation.28 | convolution fusion | flops 2165309440 | bytes 11042816 | tf_op jit(solution)/shard_map/fpd,dc->fpc/dot_general | solution.py:21
  62.5 2.9 copy.17
  65.5 18.7 %all-to-all-done.2 = bf16[4,1024,256]{2,0,1:T(4,128)(2,1)} async-done(((bf16[4,1024,256]{2,0,1:T(4,128)(2,1)}), bf16[4,1024,256]{2,0,1:T(4,128)(2,1)}, u32[]{:S(2)}, u32[]{:S(2)}) %all-to-all-start.2) | async-done | bytes 2097184 | tf_op jit(solution)/shard_map/all_to_all | solution.py:49
  84.1 4.4 %all-to-all-start = ((bf16[4,1024,256]{2,0,1:T(4,128)(2,1)}), bf16[4,1024,256]{2,0,1:T(4,128)(2,1)}, u32[]{:S(2)}, u32[]{:S(2)}) async-start(bf16[4,1024,256]{2,0,1:T(4,128)(2,1)} %copy.17), calls=%async_computation | async-start | bytes 4194304 | tf_op jit(solution)/shard_map/all_to_all | solution.py:51
  88.5 0.2 reduce-scatter.2.cloned.1.call-start
  88.7 2.0 copy.42
  90.7 3.3 reshape.30
  94.0 2.0 copy.41
  95.9 3.2 reshape.31
  99.2 8.3 %fusion.18 = f32[512,32,32]{2,1,0:T(8,128)S(1)} fusion(bf16[32,512,64]{2,1,0:T(8,128)(2,1)} %reshape.31, bf16[32,512,64]{2,1,0:T(8,128)(2,1)} %reshape.30), kind=kOutput, calls=%fused_computation.19 | convolution fusion | flops 67108864 | bytes 6291456 | tf_op jit(solution)/shard_map/fmd,gmd->fgm/dot_general | solution.py:32
  107.5 6.1 %fusion.39 = (f32[32,512]{0,1:T(8,128)S(1)}, f32[32,32,512]{0,1,2:T(8,128)}) fusion(f32[512,32,32]{2,1,0:T(8,128)S(1)} %fusion.18), kind=kOutput, calls=%fused_computation.38 | output fusion | flops 2097183 | bytes 4259840 | tf_op jit(solution)/shard_map/sub | solution.py:36
  113.6 1.5 all-to-all-done
  115.1 2.0 copy.43
  117.1 3.3 %reshape.29 = bf16[32,512,64]{2,1,0:T(8,128)(2,1)} reshape(bf16[8,4,128,256]{3,2,1,0:T(8,128)(2,1)S(1)} %bitcast.50) | data formatting | bytes 4194304 | tf_op jit(solution)/shard_map/reshape | solution.py:31
  120.4 8.1 %convert_bitcast_fusion = bf16[32,512,64]{2,0,1:T(8,128)(2,1)S(1)} fusion(f32[32,32,512]{0,1,2:T(8,128)} %get-tuple-element.6, f32[32,512]{0,1:T(8,128)S(1)} %get-tuple-element.5, bf16[32,512,64]{2,1,0:T(8,128)(2,1)} %reshape.29), kind=kOutput, calls=%fused_computation.22 | convolution fusion | flops 69206016 | bytes 6356992 | tf_op jit(solution)/shard_map/fgm,gmd->fmd/dot_general | solution.py:38
  128.5 3.6 %copy.27 = bf16[32,512,64]{2,1,0:T(8,128)(2,1)} copy(bf16[32,512,64]{2,0,1:T(8,128)(2,1)S(1)} %convert_bitcast_fusion) | data formatting | bytes 4194304 | tf_op jit(solution)/shard_map/convert_element_type | solution.py:39
  132.1 5.5 %reshape.32 = bf16[32,128,256]{2,1,0:T(8,128)(2,1)S(1)} reshape(bf16[32,512,64]{2,1,0:T(8,128)(2,1)} %copy.27) | data formatting | bytes 4194304 | tf_op jit(solution)/shard_map/reshape | solution.py:39
  137.6 5.6 %convolution_convert_fusion = bf16[32,128,1024]{2,1,0:T(8,128)(2,1)} fusion(bf16[32,128,256]{2,1,0:T(8,128)(2,1)S(1)} %reshape.32, bf16[256,1024]{1,0:T(8,128)(2,1)S(1)} %copy-done), kind=kOutput, calls=%fused_computation.13 | convolution fusion | flops 2151677952 | bytes 11010048 | tf_op jit(solution)/shard_map/fpc,cd->fpd/dot_general | solution.py:54
  143.1 0.0 reduce-scatter.2.cloned.1.call-update
  143.2 144.7 %reduce-scatter.2.cloned.1.call-done = bf16[32,128,256]{2,1,0:T(8,128)(2,1)} async-done(((bf16[32,128,1024]{2,1,0:T(8,128)(2,1)}), bf16[32,128,256]{2,1,0:T(8,128)(2,1)}) %reduce-scatter.2.cloned.1.call-update) | async-done | bytes 2097168 | tf_op jit(solution)/shard_map/reduce_scatter | solution.py:55
  287.8 30.2 %all_to_all.63 = bf16[32,128,256]{2,1,0:T(8,128)(2,1)S(1)} all-to-all(bf16[32,128,256]{2,1,0:T(8,128)(2,1)} %reduce-scatter.2.cloned.1.call-done), channel_id=1, replica_groups=mesh['seq'=8,'head'=4] {'seq'}, dimensions={0} | all-to-all | bytes 4194304 | tf_op jit(solution)/shard_map/all_to_all | solution.py:58
  318.0 1.5 copy.28
  (13 shorter events, 0.0 us)
Async XLA Ops:
  6.5 131.0 %copy-start = (bf16[256,1024]{1,0:T(8,128)(2,1)S(1)}, bf16[256,1024]{1,0:T(8,128)(2,1)}, u32[]{:S(2)}) copy-start(bf16[256,1024]{1,0:T(8,128)(2,1)} %param.9) | copy-start | bytes 1572868
  6.5 5.8 %copy-start.1 = (bf16[4,1024,1024]{2,1,0:T(8,128)(2,1)S(1)}, bf16[4,1024,1024]{2,1,0:T(8,128)(2,1)}, u32[]{:S(2)}) copy-start(bf16[4,1024,1024]{2,1,0:T(8,128)(2,1)} %param.5) | copy-start | bytes 25165828
  6.5 8.6 %copy-start.3 = (bf16[1024,256]{1,0:T(8,128)(2,1)S(1)}, bf16[1024,256]{1,0:T(8,128)(2,1)}, u32[]{:S(2)}) copy-start(bf16[1024,256]{1,0:T(8,128)(2,1)} %param.7) | copy-start | bytes 1572868
  18.3 8.2 %copy-start.4 = (bf16[1024,256]{1,0:T(8,128)(2,1)S(1)}, bf16[1024,256]{1,0:T(8,128)(2,1)}, u32[]{:S(2)}) copy-start(bf16[1024,256]{1,0:T(8,128)(2,1)} %param.6) | copy-start | bytes 1572868
  21.3 31.8 %all-to-all-start.1 = ((bf16[4,1024,256]{2,0,1:T(4,128)(2,1)}), bf16[4,1024,256]{2,0,1:T(4,128)(2,1)S(1)}, u32[]{:S(2)}, u32[]{:S(2)}) async-start(bf16[4,1024,256]{2,0,1:T(4,128)(2,1)} %copy.19), calls=%async_computation.1 | async-start | bytes 4194304 | tf_op jit(solution)/shard_map/all_to_all | solution.py:50
  31.5 25.9 %copy-start.5 = (bf16[1024,256]{1,0:T(8,128)(2,1)S(1)}, bf16[1024,256]{1,0:T(8,128)(2,1)}, u32[]{:S(2)}) copy-start(bf16[1024,256]{1,0:T(8,128)(2,1)} %param.8) | copy-start | bytes 1572868
  53.1 9.4 %copy-start.2 = (bf16[4,1024,256]{2,0,1:T(4,128)(2,1)}, bf16[4,1024,256]{2,0,1:T(4,128)(2,1)S(1)}, u32[]{:S(2)}) copy-start(bf16[4,1024,256]{2,0,1:T(4,128)(2,1)S(1)} %all-to-all-done.1) | copy-start | bytes 6291460
  53.1 31.0 %all-to-all-start.2 = ((bf16[4,1024,256]{2,0,1:T(4,128)(2,1)}), bf16[4,1024,256]{2,0,1:T(4,128)(2,1)}, u32[]{:S(2)}, u32[]{:S(2)}) async-start(bf16[4,1024,256]{2,0,1:T(4,128)(2,1)} %copy.21), calls=%async_computation.2 | async-start | bytes 4194304 | tf_op jit(solution)/shard_map/all_to_all | solution.py:49
  84.1 31.0 %all-to-all-start = ((bf16[4,1024,256]{2,0,1:T(4,128)(2,1)}), bf16[4,1024,256]{2,0,1:T(4,128)(2,1)}, u32[]{:S(2)}, u32[]{:S(2)}) async-start(bf16[4,1024,256]{2,0,1:T(4,128)(2,1)} %copy.17), calls=%async_computation | async-start | bytes 4194304 | tf_op jit(solution)/shard_map/all_to_all | solution.py:51
  88.5 199.3 %reduce-scatter.2.cloned.1.call-start = ((), (), s32[]{:S(2)}) async-start(), calls=%async_computation.5 | async-start | bytes 10485760 | tf_op jit(solution)/shard_map/reduce_scatter | solution.py:55
Sparse Core Ops, SparseCore 0:
  143.3 144.4 reduce-scatter.1
where the time goes:
time: 327 us; the launch traced here: 326 us
  waiting for transfers between devices  184 us (56%)
  local copies, waits for them, and re-layouts  36.1 us (11%)
  matrix products  35.2 us (11%)
  blocking collectives  30.2 us (9%)
  starting transfers between devices  14.1 us (4%)
  other arithmetic  13.6 us (4%)
  between operations  13.6 us (4%)
    reduce_scatter x1, waiting for transfers between devices, local(): lax.psum_scatter(partial_value.astype(jnp.bfloat16), 'head', scatter_dime...  145 us
    all_to_all x1, blocking collectives, local(): lax.all_to_all(columns, 'seq', split_axis=0, concat_axis=1, tiled=True)  30.2 us
    all_to_all x1, waiting for transfers between devices, local(): lax.all_to_all(local_query, 'seq', split_axis=1, concat_axis=0, tiled=True)  18.7 us
    all_to_all x1, waiting for transfers between devices, local(): lax.all_to_all(local_key, 'seq', split_axis=1, concat_axis=0, tiled=True)  18.6 us
    dot_general x3, matrix products, project(): jnp.einsum('fpd,dc->fpc', source, weight, preferred_element_type=jnp.floa...  13.2 us
    convert_element_type x3, local copies, waits for them, and re-layouts, project(): jnp.einsum('fpd,dc->fpc', source, weight, preferred_element_type=jnp.floa...  8.83 us
    dot_general x1, matrix products, attend(): jnp.einsum('fmd,gmd->fgm', query_flat, key_flat, preferred_element_type=j...  8.29 us
    dot_general x1, matrix products, attend(): jnp.einsum('fgm,gmd->fmd', weights, value_flat, preferred_element_type=jn...  8.14 us
  transfers between devices with their start and end apart: 4, of which 4 were waited for; matrix products, arithmetic and copies ran while one was open for 12% of the time, Pallas kernels for 0%

commit v1 on v0

--- a/solution.py
+++ b/solution.py
@@ -17,12 +17,6 @@
     return (centered * lax.rsqrt(row_var + epsilon)).astype(jnp.bfloat16)
 
 
-def project(source, weight):
-    return jnp.einsum("fpd,dc->fpc", source, weight, preferred_element_type=jnp.float32).astype(
-        jnp.bfloat16
-    )
-
-
 def attend(queries, key_rows, value_rows, head_count):
     frames, patch_count, feature_width = queries.shape
     head_size = feature_width // head_count
@@ -40,22 +34,40 @@
 
 
 def local(tokens, w_query, w_key, w_value, w_out):
-    normed = normalize(tokens)
-    head_count = w_query.shape[1] // HS
-    local_query = project(normed, w_query)
-    local_key = project(normed, w_key)
-    local_value = project(normed, w_value)
-    queries, key_rows, value_rows = (
-        lax.all_to_all(local_query, "seq", split_axis=1, concat_axis=0, tiled=True),
-        lax.all_to_all(local_key, "seq", split_axis=1, concat_axis=0, tiled=True),
-        lax.all_to_all(local_value, "seq", split_axis=1, concat_axis=0, tiled=True),
+    seq, head = lax.axis_size("seq"), lax.axis_size("head")
+    row, column = lax.axis_index("seq"), lax.axis_index("head")
+    quarter = tokens.shape[1] // head
+    own = lax.dynamic_slice_in_dim(tokens, column * quarter, quarter, axis=1)
+    width, group = w_query.shape
+    stacked = jnp.stack(
+        [
+            lax.dynamic_slice_in_dim(w, row * (width // seq), width // seq, axis=0)
+            for w in (w_query, w_key, w_value)
+        ]
     )
-    attended = attend(queries, key_rows, value_rows, head_count)
-    partial_value = jnp.einsum("fpc,cd->fpd", attended, w_out, preferred_element_type=jnp.float32)
-    columns = lax.psum_scatter(
-        partial_value.astype(jnp.bfloat16), "head", scatter_dimension=2, tiled=True
+    weights = lax.all_gather(stacked, ("head", "seq"))
+    weights = weights.reshape(head, seq, 3, width // seq, group)
+    share = w_out.shape[0] // seq
+    out_part = lax.dynamic_slice_in_dim(w_out, row * share, share, axis=0)
+    out_all = lax.all_gather(out_part, ("head", "seq"), axis=0, tiled=True)
+    mine = lax.all_to_all(own, "seq", split_axis=1, concat_axis=0, tiled=True)
+    frames, patches, _ = mine.shape
+    normed = normalize(mine)
+
+    def project(index):
+        w = weights[:, :, index].transpose(1, 2, 0, 3).reshape(width, head * group)
+        flat = jnp.dot(
+            normed.reshape(frames * patches, width), w, preferred_element_type=jnp.float32
+        )
+        return flat.astype(jnp.bfloat16).reshape(frames, patches, head * group)
+
+    attended = attend(project(0), project(1), project(2), head * group // HS)
+    mixed = jnp.dot(
+        attended.reshape(frames * patches, head * group), out_all, preferred_element_type=jnp.float32
     )
-    return lax.all_to_all(columns, "seq", split_axis=0, concat_axis=1, tiled=True)
+    mixed = mixed.astype(jnp.bfloat16).reshape(frames, patches, width)
+    mixed = lax.all_to_all(mixed, "seq", split_axis=0, concat_axis=1, tiled=True)
+    return lax.all_to_all(mixed, "head", split_axis=2, concat_axis=1, tiled=True)
 
 
 def solution(mesh):

time: 327 us -> 271 us (0.83)
  waiting for transfers between devices: 184 us -> 63.1 us
  blocking collectives: 30.2 us -> 80.6 us
  local copies, waits for them, and re-layouts: 36.1 us -> 60.4 us
  starting transfers between devices: 14.1 us -> 5.24 us
  other arithmetic: 13.6 us -> 8.68 us
    reduce_scatter x1 -> x0, waiting for transfers between devices: 145 us -> none  [local(): lax.psum_scatter(partial_value.astype(jnp.bfloat16), 'head', scatter_dime...]
    all_to_all x1 -> x2, blocking collectives: 30.2 us -> 80.6 us  [the longest x1 51.5 us: local(): lax.all_to_all(mixed, 'head', split_axis=2, concat_axis=1, tiled=True)]
    all_gather x0 -> x2, waiting for transfers between devices: none -> 35.9 us  [the longest x1 35.8 us: local(): weights = lax.all_gather(stacked, ('head', 'seq'))]
    another operation x0 -> x6, local copies, waits for them, and re-layouts: none -> 23.1 us  [the longest x1 6.39 us: attend(): query_flat = queries.reshape(frames, patch_count * head_count, head_size)]
    transpose x0 -> x4, local copies, waits for them, and re-layouts: none -> 16.8 us  [project(): w = weights[:, :, index].transpose(1, 2, 0, 3).reshape(width, head * group)]
    reshape x4 -> x0, local copies, waits for them, and re-layouts: 15.2 us -> none  [the longest x1 5.48 us: attend(): attended.astype(jnp.bfloat16).reshape(frames, patch_count, feature_width)]
    all_to_all x3 -> x1, waiting for transfers between devices: 38.8 us -> 27.2 us  [local(): mine = lax.all_to_all(own, 'seq', split_axis=1, concat_axis=0, tiled=True)]
    all_to_all x3 -> x1, starting transfers between devices: 13.9 us -> 5.2 us  [local(): mine = lax.all_to_all(own, 'seq', split_axis=1, concat_axis=0, tiled=True)]
  transfers between devices with their start and end apart: 4 -> 3, of which waited for: 4 -> 2; matrix products, arithmetic and copies ran while one was open for 12% -> 35% of each run, Pallas kernels for 0% -> 0%
where the time goes in v1:
time: 271 us; the launch traced here: 270 us
  blocking collectives  80.6 us (30%)
  waiting for transfers between devices  63.1 us (23%)
  local copies, waits for them, and re-layouts  60.4 us (22%)
  matrix products  38.1 us (14%)
  between operations  13.5 us (5%)
  other arithmetic  8.68 us (3%)
  starting transfers between devices  5.24 us (2%)
    all_to_all x1, blocking collectives, local(): lax.all_to_all(mixed, 'head', split_axis=2, concat_axis=1, tiled=True)  51.5 us
    all_gather x1, waiting for transfers between devices, local(): weights = lax.all_gather(stacked, ('head', 'seq'))  35.8 us
    all_to_all x1, blocking collectives, local(): lax.all_to_all(mixed, 'seq', split_axis=0, concat_axis=1, tiled=True)  29.1 us
    all_to_all x1, waiting for transfers between devices, local(): mine = lax.all_to_all(own, 'seq', split_axis=1, concat_axis=0, tiled=True)  27.2 us
    dot_general x3, matrix products, project(): jnp.dot(normed.reshape(frames * patches, width), w, preferred_element_typ...  16.8 us
    transpose x4, local copies, waits for them, and re-layouts, project(): w = weights[:, :, index].transpose(1, 2, 0, 3).reshape(width, head * group)  16.8 us
    dot_general x1, matrix products, attend(): jnp.einsum('fgm,gmd->fmd', weights, value_flat, preferred_element_type=jn...  9.11 us
    dot_general x1, matrix products, attend(): jnp.einsum('fmd,gmd->fgm', query_flat, key_flat, preferred_element_type=j...  8.33 us
  transfers between devices with their start and end apart: 3, of which 2 were waited for; matrix products, arithmetic and copies ran while one was open for 35% of the time, Pallas kernels for 0%

profile of v1, /device:TPU:0, one launch (start us, length us, event | category | flops | bytes accessed | tf_op | source)
XLA Modules:
  0.0 269.6 jit_solution(12941206944487016885)
XLA Ops:
  6.5 1.0 copy-done
  7.6 0.9 dynamic-slice_bitcast_fusion
  8.5 0.7 pad_maximum_fusion
  9.2 1.8 constant_dynamic-slice_fusion.1
  11.0 2.9 %copy.44 = bf16[4,256,1024]{2,0,1:T(4,128)(2,1)} copy(bf16[4,256,1024]{2,1,0:T(8,128)(2,1)S(1)} %constant_dynamic-slice_fusion.1) | data formatting | bytes 4194304
  13.9 5.2 %all-to-all-start = ((bf16[4,256,1024]{2,0,1:T(4,128)(2,1)}), bf16[4,256,1024]{2,0,1:T(4,128)(2,1)S(1)}, u32[]{:S(2)}, u32[]{:S(2)}) async-start(bf16[4,256,1024]{2,0,1:T(4,128)(2,1)} %copy.44), calls=%async_computation | async-start | bytes 4194304 | tf_op jit(solution)/shard_map/all_to_all | solution.py:53
  19.2 1.5 constant_dynamic-slice_fusion
  20.7 27.2 %all-to-all-done = bf16[4,256,1024]{2,0,1:T(4,128)(2,1)S(1)} async-done(((bf16[4,256,1024]{2,0,1:T(4,128)(2,1)}), bf16[4,256,1024]{2,0,1:T(4,128)(2,1)S(1)}, u32[]{:S(2)}, u32[]{:S(2)}) %all-to-all-start) | async-done | bytes 2097184 | tf_op jit(solution)/shard_map/all_to_all | solution.py:53
  48.9 0.7 fusion.11
  49.6 0.8 fusion.12
  50.4 1.5 copy.30
  51.9 35.8 %all-gather.6.cloned.1.call-done = bf16[96,128,256]{2,1,0:T(8,128)(2,1)} async-done(((bf16[3,128,256]{2,1,0:T(8,128)(2,1)}), bf16[96,128,256]{2,1,0:T(8,128)(2,1)}) %all-gather.6.cloned.1.call-update) | async-done | bytes 6291472 | tf_op jit(solution)/shard_map/all_gather | solution.py:48
  87.7 5.6 %slice_bitcast_fusion.2 = (bf16[8,128,4,256]{3,1,0,2:T(8,128)(2,1)S(1)}, bf16[8,128,4,256]{3,1,0,2:T(8,128)(2,1)}, bf16[8,128,4,256]{3,1,0,2:T(8,128)(2,1)}) fusion(bf16[4,8,3,128,256]{4,3,2,1,0:T(8,128)(2,1)} %bitcast.96), kind=kLoop, calls=%fused_computation.33 | loop fusion | bytes 12582912 | tf_op jit(solution)/shard_map/transpose | solution.py:58
  93.2 4.3 %copy.32 = bf16[8,128,4,256]{1,0,3,2:T(8,128)(2,1)} copy(bf16[8,128,4,256]{3,1,0,2:T(8,128)(2,1)} %get-tuple-element.7) | data formatting | bytes 4194304 | tf_op jit(solution)/shard_map/transpose | solution.py:58
  97.6 5.9 %fusion.33 = bf16[1024,1024]{1,0:T(8,128)(2,1)} fusion(bf16[1024,1024]{1,0:T(8,128)(2,1)} %bitcast.97, bf16[128,8,8,128]{3,2,1,0:T(8,128)(2,1)} %bitcast.102), kind=kOutput, calls=%fused_computation.35 | convolution fusion | flops 2148532224 | bytes 6291456 | tf_op jit(solution)/shard_map/dot_general | solution.py:59
  103.5 6.4 %reshape_reshape.13 = bf16[32,512,64]{2,1,0:T(8,128)(2,1)} reshape(bf16[1024,1024]{1,0:T(8,128)(2,1)} %fusion.33) | data formatting | bytes 4194304 | tf_op jit(solution)/shard_map/reshape;reshape | solution.py:24
  109.9 4.3 %copy.33 = bf16[8,128,4,256]{1,0,3,2:T(8,128)(2,1)} copy(bf16[8,128,4,256]{3,1,0,2:T(8,128)(2,1)} %get-tuple-element.6) | data formatting | bytes 4194304 | tf_op jit(solution)/shard_map/transpose | solution.py:58
  114.1 6.0 %fusion.36 = bf16[1024,1024]{1,0:T(8,128)(2,1)} fusion(bf16[1024,1024]{1,0:T(8,128)(2,1)} %bitcast.98, bf16[128,8,8,128]{3,2,1,0:T(8,128)(2,1)} %bitcast.103), kind=kOutput, calls=%fused_computation.36 | convolution fusion | flops 2148532224 | bytes 6291456 | tf_op jit(solution)/shard_map/dot_general | solution.py:59
  120.1 6.4 %reshape_reshape.14 = bf16[32,512,64]{2,1,0:T(8,128)(2,1)} reshape(bf16[1024,1024]{1,0:T(8,128)(2,1)} %fusion.36) | data formatting | bytes 4194304 | tf_op jit(solution)/shard_map/reshape;reshape | solution.py:23
  126.5 2.6 copy.31
  129.1 4.9 %fusion.30 = bf16[1024,1024]{1,0:T(8,128)(2,1)S(1)} fusion(bf16[1024,1024]{1,0:T(8,128)(2,1)} %bitcast.99, bf16[128,8,8,128]{3,2,1,0:T(8,128)(2,1)} %bitcast.100), kind=kOutput, calls=%fused_computation.34 | convolution fusion | flops 2148532224 | bytes 6291456 | tf_op jit(solution)/shard_map/dot_general | solution.py:59
  134.0 4.0 %reshape_reshape.12 = bf16[32,512,64]{2,1,0:T(8,128)(2,1)} reshape(bf16[1024,1024]{1,0:T(8,128)(2,1)S(1)} %fusion.30) | data formatting | bytes 4194304 | tf_op jit(solution)/shard_map/reshape;reshape | solution.py:25
  138.0 8.3 %fusion.14 = f32[512,32,32]{2,1,0:T(8,128)S(1)} fusion(bf16[32,512,64]{2,1,0:T(8,128)(2,1)} %reshape_reshape.14, bf16[32,512,64]{2,1,0:T(8,128)(2,1)} %reshape_reshape.13), kind=kOutput, calls=%fused_computation.16 | convolution fusion | flops 67108864 | bytes 6291456 | tf_op jit(solution)/shard_map/fmd,gmd->fgm/dot_general | solution.py:26
  146.3 6.1 %fusion.40 = (f32[32,512]{0,1:T(8,128)S(1)}, f32[32,32,512]{0,1,2:T(8,128)}) fusion(f32[512,32,32]{2,1,0:T(8,128)S(1)} %fusion.14), kind=kOutput, calls=%fused_computation.47 | output fusion | flops 2097183 | bytes 4259840 | tf_op jit(solution)/shard_map/sub | solution.py:30
  152.5 9.1 %convert_bitcast_fusion.1 = bf16[32,512,64]{2,0,1:T(8,128)(2,1)} fusion(f32[32,32,512]{0,1,2:T(8,128)} %get-tuple-element.9, f32[32,512]{0,1:T(8,128)S(1)} %get-tuple-element.8, bf16[32,512,64]{2,1,0:T(8,128)(2,1)S(1)} %copy-done.2), kind=kOutput, calls=%fused_computation.19 | convolution fusion | flops 69206016 | bytes 6356992 | tf_op jit(solution)/shard_map/fgm,gmd->fmd/dot_general | solution.py:32
  161.6 5.7 %copy.38 = bf16[32,512,64]{2,1,0:T(8,128)(2,1)} copy(bf16[32,512,64]{2,0,1:T(8,128)(2,1)} %convert_bitcast_fusion.1) | data formatting | bytes 4194304 | tf_op jit(solution)/shard_map/convert_element_type | solution.py:33
  167.3 5.5 %reshape_reshape.15 = bf16[1024,1024]{1,0:T(8,128)(2,1)S(1)} reshape(bf16[32,512,64]{2,1,0:T(8,128)(2,1)} %copy.38) | data formatting | bytes 4194304 | tf_op jit(solution)/shard_map/reshape;reshape | solution.py:66
  172.8 3.9 %convolution_convert_fusion = bf16[1024,1024]{1,0:T(8,128)(2,1)S(1)} fusion(bf16[1024,1024]{1,0:T(8,128)(2,1)S(1)} %reshape_reshape.15, bf16[1024,1024]{1,0:T(8,128)(2,1)} %all-gather.4.cloned.1.call-done), kind=kOutput, calls=%fused_computation.37 | convolution fusion | flops 2148532224 | bytes 6291456 | tf_op jit(solution)/shard_map/dot_general | solution.py:65
  176.8 29.1 %all_to_all.45 = bf16[32,32,1024]{2,1,0:T(8,128)(2,1)S(1)} all-to-all(bf16[32,32,1024]{2,1,0:T(8,128)(2,1)S(1)} %bitcast.101), channel_id=1, replica_groups=mesh['seq'=8,'head'=4] {'seq'}, dimensions={0} | all-to-all | bytes 4194304 | tf_op jit(solution)/shard_map/all_to_all | solution.py:69
  206.1 2.6 copy.40
  208.7 51.5 %all_to_all.46 = bf16[4,256,1024]{1,0,2:T(4,128)(2,1)S(1)} all-to-all(bf16[4,256,1024]{1,0,2:T(4,128)(2,1)} %copy.40), channel_id=1, replica_groups=mesh['seq'=8,'head'=4] {'head'}, dimensions={2} | all-to-all | bytes 4194304 | tf_op jit(solution)/shard_map/all_to_all | solution.py:70
  260.4 2.3 copy.42
  (17 shorter events, 1.5 us)
Async XLA Ops:
  6.5 1.0 copy-start
  6.5 81.2 %all-gather.6.cloned.1.call-start = ((), (), s32[]{:S(2)}) async-start(), calls=%async_computation.4 | async-start | bytes 6488064 | tf_op jit(solution)/shard_map/all_gather | solution.py:48
  13.9 33.9 %all-to-all-start = ((bf16[4,256,1024]{2,0,1:T(4,128)(2,1)}), bf16[4,256,1024]{2,0,1:T(4,128)(2,1)S(1)}, u32[]{:S(2)}, u32[]{:S(2)}) async-start(bf16[4,256,1024]{2,0,1:T(4,128)(2,1)} %copy.44), calls=%async_computation | async-start | bytes 4194304 | tf_op jit(solution)/shard_map/all_to_all | solution.py:53
  19.1 153.7 %all-gather.4.cloned.1.call-start = ((), (), s32[]{:S(2)}) async-start(), calls=%async_computation.3 | async-start | bytes 2162688 | tf_op jit(solution)/shard_map/all_gather | solution.py:52
  146.3 6.1 %copy-start.2 = (bf16[32,512,64]{2,1,0:T(8,128)(2,1)S(1)}, bf16[32,512,64]{2,1,0:T(8,128)(2,1)}, u32[]{:S(2)}) copy-start(bf16[32,512,64]{2,1,0:T(8,128)(2,1)} %reshape_reshape.12) | copy-start | bytes 6291460
  260.4 2.4 copy-start.1
Sparse Core Ops, SparseCore 0:
  10.2 77.4 all-gather.5
  90.5 54.7 all-gather.3

commit v2 on v0

v2 whole, which is shorter than its diff:
```python
import functools

import jax
import jax.numpy as jnp
from jax import lax
from jax.experimental import pallas as pl
from jax.experimental.pallas import tpu as pltpu
from jax.sharding import PartitionSpec as P

HS = 64
EPSILON = 1e-05
SUB = 8
MASKED = -1e30
MESH = pl.DeviceIdType.MESH


def drain(ref, sem):
    pltpu.make_async_copy(ref, ref, sem).wait()


def kernel(
    seq, head,
    tok, wq, wk, wv, wo, out,
    x, normed, qkv, w, w_o, att, mixed, bias,
    tok_send, tok_recv, load_sem, s1_send, s1_recv, s2_send, s2_recv, s3_send, s3_recv,
    o1_send, o1_recv, o2_send, o2_recv, out_send, out_recv,
):
    s, z = lax.axis_index("seq"), lax.axis_index("head")
    groups, frames = x.shape[0], x.shape[1]
    own_frames = tok.shape[0]
    width = tok.shape[2]
    columns = wq.shape[1]
    rows = frames * SUB
    own_patches = groups * SUB
    quarter = seq * own_patches
    slice_rows = width // seq
    half_seq = seq // 2
    parity, place = lax.rem(s, 2), s // 2
    sibling = s + 1 - 2 * parity
    total = seq * head

    def send(src, dst, send_sem, recv_sem, to_s, to_z):
        pltpu.make_async_remote_copy(
            src_ref=src, dst_ref=dst, send_sem=send_sem, recv_sem=recv_sem,
            device_id=(to_s, to_z), device_id_type=MESH,
        ).start()

    def tok_block(to_s, g):
        start = pl.multiple_of(z * quarter + to_s * own_patches + g * SUB, SUB)
        return tok.at[:, pl.ds(start, SUB), :]

    slice_start = pl.multiple_of((parity * half_seq + place) * slice_rows, slice_rows)
    my_slice = pl.ds(slice_start, slice_rows)
    weights = (wq, wk, wv)
    for j in range(3):
        for i in range(1, head):
            send(
                weights[j].at[my_slice, :], w.at[j, z, my_slice, :],
                s1_send.at[j], s1_recv.at[j, i - 1], s, lax.rem(z + i, head),
            )
    for i in range(1, seq):
        to_s = lax.rem(s + i, seq)
        for g in range(groups):
            send(
                tok_block(to_s, g), x.at[g, pl.ds(s * own_frames, own_frames)],
                tok_send.at[g], tok_recv.at[g], to_s, z,
            )
    for g in range(groups):
        pltpu.make_async_copy(
            tok_block(s, g), x.at[g, pl.ds(s * own_frames, own_frames)], tok_recv.at[g]
        ).start()
    shard = width // head
    half = shard // 2
    for i in range(1, head):
        send(
            wo.at[pl.ds(pl.multiple_of(parity * half, half), half), :],
            w_o.at[pl.ds(pl.multiple_of(z * shard + parity * half, half), half), :],
            o1_send, o1_recv.at[i - 1], s, lax.rem(z + i, head),
        )
    own = [pltpu.make_async_copy(weights[j], w.at[j, z], load_sem.at[j]) for j in range(3)]
    own.append(
        pltpu.make_async_copy(
            wo, w_o.at[pl.ds(pl.multiple_of(z * shard, shard), shard), :], load_sem.at[3]
        )
    )
    for copy in own:
        copy.start()

    row = lax.broadcasted_iota(jnp.int32, (rows, rows), 0)
    col = lax.broadcasted_iota(jnp.int32, (rows, rows), 1)
    bias[...] = jnp.where((row & (SUB - 1)) == (col & (SUB - 1)), 0.0, MASKED)

    for j in range(3):
        for i in range(1, head):
            from_z = lax.rem(z + head - i, head)
            piece = w.at[j, from_z, my_slice, :]
            drain(piece, s1_recv.at[j, i - 1])
            for k in range(1, half_seq):
                to_s = lax.rem(place + k, half_seq) * 2 + parity
                send(piece, piece, s2_send.at[j], s2_recv.at[j], to_s, z)

    step_frames = 8
    for g in range(groups):
        drain(x.at[g], tok_recv.at[g])

        @pl.loop(0, frames // step_frames)
        def _(c):
            block = x[g, pl.ds(c * step_frames, step_frames)].astype(jnp.float32)
            values = block.reshape(step_frames * SUB, width)
            mean = jnp.mean(values, axis=-1, keepdims=True)
            centered = values - mean
            var = jnp.mean(centered * centered, axis=-1, keepdims=True)
            start = pl.multiple_of(c * step_frames * SUB, step_frames * SUB)
            normed[g, pl.ds(start, step_frames * SUB), :] = (
                centered * lax.rsqrt(var + EPSILON)
            ).astype(jnp.bfloat16)

    def project(j, g):
        @pl.loop(0, head)
        def _(h):
            r = jnp.dot(normed[g], w[j, h], preferred_element_type=jnp.float32)
            if j == 0:
                r = r * HS ** (-0.5)
            start = pl.multiple_of(h * columns, columns)
            qkv[j, g, :, pl.ds(start, columns)] = r.astype(jnp.bfloat16)

    parity_rows = pl.ds(
        pl.multiple_of(parity * half_seq * slice_rows, slice_rows), half_seq * slice_rows
    )
    for j in range(3):
        own[j].wait()
        drain(
            w.at[j, pl.ds(0, head - 1), pl.ds(0, (half_seq - 1) * slice_rows), :], s2_recv.at[j]
        )
        for i in range(1, head):
            piece = w.at[j, lax.rem(z + i, head), parity_rows, :]
            send(piece, piece, s3_send.at[j], s3_recv.at[j], sibling, z)
        if j == 1:
            for i in range(1, head):
                from_z = lax.rem(z + head - i, head)
                piece = w_o.at[
                    pl.ds(pl.multiple_of(from_z * shard + parity * half, half), half), :
                ]
                drain(piece, o1_recv.at[i - 1])
                send(piece, piece, o2_send, o2_recv, sibling, z)
        drain(w.at[j, pl.ds(0, head - 1), pl.ds(0, half_seq * slice_rows), :], s3_recv.at[j])
        if j < 2:

            @pl.loop(0, groups)
            def _(g):
                project(j, g)

    own[3].wait()
    drain(w_o.at[pl.ds(0, (head - 1) * half), :], o2_recv)

    pair = 2 * HS
    left = lax.broadcasted_iota(jnp.int32, (rows, pair), 1) < HS
    left_b = left.astype(jnp.float32).astype(jnp.bfloat16)
    right_b = (1.0 - left.astype(jnp.float32)).astype(jnp.bfloat16)
    ones = jnp.ones((rows, pair), jnp.bfloat16)
    me = s * head + z

    def out_block(g):
        start = pl.multiple_of(z * quarter + s * own_patches + g * SUB, SUB)
        return out.at[:, pl.ds(start, SUB), :]

    @pl.loop(0, groups)
    def _(g):
        project(2, g)

        @pl.loop(0, width // pair)
        def _(n):
            lanes = pl.ds(pl.multiple_of(n * pair, pair), pair)
            q, k, v = qkv[0, g, :, lanes], qkv[1, g, :, lanes], qkv[2, g, :, lanes]
            v_ones = jnp.concatenate([v, ones], axis=1)
            results = []
            for mask in (left_b, right_b):
                score = lax.dot_general(
                    q * mask, k, (((1,), (1,)), ((), ())), preferred_element_type=jnp.float32
                )
                score = score + bias[...]
                top = jnp.max(score, axis=1, keepdims=True)
                raised = jnp.exp(score - top).astype(jnp.bfloat16)
                r = jnp.dot(raised, v_ones, preferred_element_type=jnp.float32)
                results.append(r[:, :pair] / r[:, pair:])
            att[:, lanes] = jnp.where(left, results[0], results[1]).astype(jnp.bfloat16)

        @pl.loop(0, head)
        def _(h):
            lanes = pl.ds(pl.multiple_of(h * columns, columns), columns)
            r = jnp.dot(att[...], w_o[:, lanes], preferred_element_type=jnp.float32)
            mixed[g, pl.ds(h * frames, frames)] = r.reshape(frames, SUB, columns).astype(
                jnp.bfloat16
            )

        @pl.loop(1, total)
        def _(i):
            to = lax.rem(me + i, total)
            to_s, to_z = to // head, lax.rem(to, head)
            send(
                mixed.at[g, pl.ds(to_z * frames + to_s * own_frames, own_frames)],
                out_block(g), out_send.at[g], out_recv, to_s, to_z,
            )

        pltpu.make_async_copy(
            mixed.at[g, pl.ds(z * frames + s * own_frames, own_frames)], out_block(g), out_recv
        ).start()

    drain(out, out_recv)
    blocks = head * frames
    for g in range(groups):
        drain(mixed.at[g, pl.ds(0, blocks - blocks // total)], out_send.at[g])
        drain(x.at[g, pl.ds(0, frames - own_frames)], tok_send.at[g])
    for j in range(3):
        drain(w.at[j, pl.ds(0, head - 1), pl.ds(0, slice_rows), :], s1_send.at[j])
        drain(
            w.at[j, pl.ds(0, head - 1), pl.ds(0, (half_seq - 1) * slice_rows), :], s2_send.at[j]
        )
        drain(w.at[j, pl.ds(0, head - 1), pl.ds(0, half_seq * slice_rows), :], s3_send.at[j])
    drain(w_o.at[pl.ds(0, (head - 1) * half), :], o1_send)
    drain(w_o.at[pl.ds(0, (head - 1) * half), :], o2_send)


def local(tokens, w_query, w_key, w_value, w_out):
    seq, head = lax.axis_size("seq"), lax.axis_size("head")
    own_frames, patches, width = tokens.shape
    frames = own_frames * seq
    groups = patches // (seq * head * SUB)
    rows = frames * SUB
    columns = w_query.shape[1]
    bf16 = jnp.bfloat16
    dma = pltpu.SemaphoreType.DMA
    return pl.pallas_call(
        functools.partial(kernel, seq, head),
        out_shape=jax.ShapeDtypeStruct((own_frames, patches, width // head), bf16),
        in_specs=[pl.BlockSpec(memory_space=pl.ANY)] * 5,
        out_specs=pl.BlockSpec(memory_space=pl.ANY),
        scratch_shapes=[
            pltpu.VMEM((groups, frames, SUB, width), bf16),
            pltpu.VMEM((groups, rows, width), bf16),
            pltpu.VMEM((3, groups, rows, width), bf16),
            pltpu.VMEM((3, head, width, columns), bf16),
            pltpu.VMEM((width, width), bf16),
            pltpu.VMEM((rows, width), bf16),
            pltpu.VMEM((groups, head * frames, SUB, width // head), bf16),
            pltpu.VMEM((rows, rows), jnp.float32),
            dma((groups,)), dma((groups,)), dma((4,)),
            dma((3,)), dma((3, head - 1)), dma((3,)), dma((3,)), dma((3,)), dma((3,)),
            dma, dma((head - 1,)), dma, dma, dma((groups,)), dma,
        ],
        compiler_params=pltpu.CompilerParams(
            has_side_effects=True, vmem_limit_bytes=60 * 1024 * 1024
        ),
    )(tokens, w_query, w_key, w_value, w_out)


def solution(mesh):
    return jax.shard_map(
        local,
        mesh=mesh,
        in_specs=(
            P("seq", None, None),
            P(None, "head"),
            P(None, "head"),
            P(None, "head"),
            P("head", None),
        ),
        out_specs=P("seq", None, "head"),
        check_vma=False,
    )
```

time: 327 us -> 118 us (0.36)
  waiting for transfers between devices: 184 us -> 0 us
  Pallas kernels: 0 us -> 115 us
  matrix products: 35.2 us -> 0 us
  local copies, waits for them, and re-layouts: 36.1 us -> 3.05 us
  blocking collectives: 30.2 us -> 0 us
  starting transfers between devices: 14.1 us -> 0 us
  other arithmetic: 13.6 us -> 0 us
  between operations: 13.6 us -> 0.01 us
    reduce_scatter x1 -> x0, waiting for transfers between devices: 145 us -> none  [local(): lax.psum_scatter(partial_value.astype(jnp.bfloat16), 'head', scatter_dime...]
    pallas_call x0 -> x1, Pallas kernels: none -> 115 us  [local(): pl.pallas_call(functools.partial(kernel, seq, head), out_shape=jax.ShapeD...]
    all_to_all x3 -> x0, waiting for transfers between devices: 38.8 us -> none  [the longest x1 18.7 us: local(): lax.all_to_all(local_query, 'seq', split_axis=1, concat_axis=0, tiled=True)]
    dot_general x6 -> x0, matrix products: 35.2 us -> none  [the longest x3 13.2 us: project(): jnp.einsum('fpd,dc->fpc', source, weight, preferred_element_type=jnp.floa...]
    all_to_all x1 -> x0, blocking collectives: 30.2 us -> none  [local(): lax.all_to_all(columns, 'seq', split_axis=0, concat_axis=1, tiled=True)]
    reshape x4 -> x0, local copies, waits for them, and re-layouts: 15.2 us -> none  [the longest x1 5.48 us: attend(): attended.astype(jnp.bfloat16).reshape(frames, patch_count, feature_width)]
    all_to_all x3 -> x0, starting transfers between devices: 13.9 us -> none  [the longest x1 5.21 us: local(): lax.all_to_all(local_key, 'seq', split_axis=1, concat_axis=0, tiled=True)]
    convert_element_type x4 -> x0, local copies, waits for them, and re-layouts: 12.4 us -> none  [the longest x3 8.83 us: project(): jnp.einsum('fpd,dc->fpc', source, weight, preferred_element_type=jnp.floa...]
  transfers between devices with their start and end apart: 4 -> 0, of which waited for: 4 -> 0; matrix products, arithmetic and copies ran while one was open for 12% -> 0% of each run, Pallas kernels for 0% -> 0%
where the time goes in v2:
time: 118 us
  Pallas kernels  115 us (97%)
  local copies, waits for them, and re-layouts  3.05 us (3%)
    pallas_call x1, Pallas kernels, local(): pl.pallas_call(functools.partial(kernel, seq, head), out_shape=jax.ShapeD...  115 us
    unnamed x1, local copies, waits for them, and re-layouts  3.05 us

profile of v2, /device:TPU:0, one launch (start us, length us, event | category | flops | bytes accessed | tf_op | source)
XLA Modules:
  0.0 117.9 jit_solution(4705984196626696231)
XLA Ops:
  0.0 114.8 %shard_map.55 = bf16[4,1024,256]{2,1,0:T(8,128)(2,1)} custom-call(bf16[4,1024,1024]{2,1,0:T(8,128)(2,1)} %tok.1, bf16[1024,256]{1,0:T(8,128)(2,1)} %wq.1, bf16[1024,256]{1,0:T(8,128)(2,1)} %wk.1, bf16[1024,256]{1,0:T(8,128)(2,1)} %wv.1, bf16[256,1024]{1,0:T(8,128)(2,1)} %wo.1), custom_call_target="tpu_custom_call" | custom-call | tf_op jit(solution)/shard_map/pallas_call | solution.py:233
  114.8 3.0 %copy.7 = bf16[4,1024,256]{2,1,0:T(8,128)(2,1)} copy(bf16[4,1024,256]{2,1,0:T(8,128)(2,1)} %shard_map.55) | data formatting | bytes 4194304

commit v3 on v2

--- a/solution.py
+++ b/solution.py
@@ -58,17 +58,18 @@
                 weights[j].at[my_slice, :], w.at[j, z, my_slice, :],
                 s1_send.at[j], s1_recv.at[j, i - 1], s, lax.rem(z + i, head),
             )
-    for i in range(1, seq):
-        to_s = lax.rem(s + i, seq)
-        for g in range(groups):
+    def exchange(g):
+        for i in range(1, seq):
+            to_s = lax.rem(s + i, seq)
             send(
                 tok_block(to_s, g), x.at[g, pl.ds(s * own_frames, own_frames)],
                 tok_send.at[g], tok_recv.at[g], to_s, z,
             )
-    for g in range(groups):
         pltpu.make_async_copy(
             tok_block(s, g), x.at[g, pl.ds(s * own_frames, own_frames)], tok_recv.at[g]
         ).start()
+
+    exchange(0)
     shard = width // head
     half = shard // 2
     for i in range(1, head):
@@ -99,8 +100,12 @@
                 to_s = lax.rem(place + k, half_seq) * 2 + parity
                 send(piece, piece, s2_send.at[j], s2_recv.at[j], to_s, z)
 
+    for g in range(1, groups):
+        exchange(g)
+
     step_frames = 8
-    for g in range(groups):
+
+    def norm(g):
         drain(x.at[g], tok_recv.at[g])
 
         @pl.loop(0, frames // step_frames)
@@ -111,18 +116,20 @@
             centered = values - mean
             var = jnp.mean(centered * centered, axis=-1, keepdims=True)
             start = pl.multiple_of(c * step_frames * SUB, step_frames * SUB)
-            normed[g, pl.ds(start, step_frames * SUB), :] = (
+            normed[pl.ds(start, step_frames * SUB), :] = (
                 centered * lax.rsqrt(var + EPSILON)
             ).astype(jnp.bfloat16)
 
-    def project(j, g):
+    norm(0)
+
+    def project(j):
         @pl.loop(0, head)
         def _(h):
-            r = jnp.dot(normed[g], w[j, h], preferred_element_type=jnp.float32)
+            r = jnp.dot(normed[...], w[j, h], preferred_element_type=jnp.float32)
             if j == 0:
                 r = r * HS ** (-0.5)
             start = pl.multiple_of(h * columns, columns)
-            qkv[j, g, :, pl.ds(start, columns)] = r.astype(jnp.bfloat16)
+            qkv[j, :, pl.ds(start, columns)] = r.astype(jnp.bfloat16)
 
     parity_rows = pl.ds(
         pl.multiple_of(parity * half_seq * slice_rows, slice_rows), half_seq * slice_rows
@@ -144,11 +151,7 @@
                 drain(piece, o1_recv.at[i - 1])
                 send(piece, piece, o2_send, o2_recv, sibling, z)
         drain(w.at[j, pl.ds(0, head - 1), pl.ds(0, half_seq * slice_rows), :], s3_recv.at[j])
-        if j < 2:
-
-            @pl.loop(0, groups)
-            def _(g):
-                project(j, g)
+        project(j)
 
     own[3].wait()
     drain(w_o.at[pl.ds(0, (head - 1) * half), :], o2_recv)
@@ -164,14 +167,11 @@
         start = pl.multiple_of(z * quarter + s * own_patches + g * SUB, SUB)
         return out.at[:, pl.ds(start, SUB), :]
 
-    @pl.loop(0, groups)
-    def _(g):
-        project(2, g)
-
+    def finish(g):
         @pl.loop(0, width // pair)
         def _(n):
             lanes = pl.ds(pl.multiple_of(n * pair, pair), pair)
-            q, k, v = qkv[0, g, :, lanes], qkv[1, g, :, lanes], qkv[2, g, :, lanes]
+            q, k, v = qkv[0, :, lanes], qkv[1, :, lanes], qkv[2, :, lanes]
             v_ones = jnp.concatenate([v, ones], axis=1)
             results = []
             for mask in (left_b, right_b):
@@ -205,6 +205,15 @@
         pltpu.make_async_copy(
             mixed.at[g, pl.ds(z * frames + s * own_frames, own_frames)], out_block(g), out_recv
         ).start()
+
+    finish(0)
+
+    @pl.loop(1, groups)
+    def _(g):
+        norm(g)
+        for j in range(3):
+            project(j)
+        finish(g)
 
     drain(out, out_recv)
     blocks = head * frames
@@ -237,8 +246,8 @@
         out_specs=pl.BlockSpec(memory_space=pl.ANY),
         scratch_shapes=[
             pltpu.VMEM((groups, frames, SUB, width), bf16),
-            pltpu.VMEM((groups, rows, width), bf16),
-            pltpu.VMEM((3, groups, rows, width), bf16),
+            pltpu.VMEM((rows, width), bf16),
+            pltpu.VMEM((3, rows, width), bf16),
             pltpu.VMEM((3, head, width, columns), bf16),
             pltpu.VMEM((width, width), bf16),
             pltpu.VMEM((rows, width), bf16),

time: 118 us -> 106 us (0.90)
  Pallas kernels: 115 us -> 103 us
    pallas_call x1, Pallas kernels: 115 us -> 103 us  [local(): pl.pallas_call(functools.partial(kernel, seq, head), out_shape=jax.ShapeD...]
where the time goes in v3:
time: 106 us
  Pallas kernels  103 us (97%)
  local copies, waits for them, and re-layouts  3.05 us (3%)
    pallas_call x1, Pallas kernels, local(): pl.pallas_call(functools.partial(kernel, seq, head), out_shape=jax.ShapeD...  103 us
    unnamed x1, local copies, waits for them, and re-layouts  3.05 us

profile of v3, /device:TPU:0, one launch (start us, length us, event | category | flops | bytes accessed | tf_op | source)
XLA Modules:
  0.0 106.1 jit_solution(5280782702417898286)
XLA Ops:
  0.0 103.0 %shard_map.55 = bf16[4,1024,256]{2,1,0:T(8,128)(2,1)} custom-call(bf16[4,1024,1024]{2,1,0:T(8,128)(2,1)} %tok.1, bf16[1024,256]{1,0:T(8,128)(2,1)} %wq.1, bf16[1024,256]{1,0:T(8,128)(2,1)} %wk.1, bf16[1024,256]{1,0:T(8,128)(2,1)} %wv.1, bf16[256,1024]{1,0:T(8,128)(2,1)} %wo.1), custom_call_target="tpu_custom_call" | custom-call | tf_op jit(solution)/shard_map/pallas_call | solution.py:242
  103.0 3.0 %copy.7 = bf16[4,1024,256]{2,1,0:T(8,128)(2,1)} copy(bf16[4,1024,256]{2,1,0:T(8,128)(2,1)} %shard_map.55) | data formatting | bytes 4194304

commit v4 on v3

--- a/solution.py
+++ b/solution.py
@@ -22,7 +22,7 @@
     seq, head,
     tok, wq, wk, wv, wo, out,
     x, normed, qkv, w, w_o, att, mixed, bias,
-    tok_send, tok_recv, load_sem, s1_send, s1_recv, s2_send, s2_recv, s3_send, s3_recv,
+    tok_send, tok_recv, load_sem, s1_send, s1_recv, s2_send, s2_recv, far_recv, s3_send, s3_recv,
     o1_send, o1_recv, o2_send, o2_recv, out_send, out_recv,
 ):
     s, z = lax.axis_index("seq"), lax.axis_index("head")
@@ -52,12 +52,22 @@
     slice_start = pl.multiple_of((parity * half_seq + place) * slice_rows, slice_rows)
     my_slice = pl.ds(slice_start, slice_rows)
     weights = (wq, wk, wv)
+    def ways(d):
+        return (
+            (z - d, z - d >= 0, z + 1, z + 1 < head),
+            (z + d, z + d < head, z - 1, z - 1 >= 0),
+        )
+
     for j in range(3):
-        for i in range(1, head):
-            send(
-                weights[j].at[my_slice, :], w.at[j, z, my_slice, :],
-                s1_send.at[j], s1_recv.at[j, i - 1], s, lax.rem(z + i, head),
-            )
+        for _, _, after, open_ in ways(1):
+
+            @pl.when(open_)
+            def _():
+                send(
+                    weights[j].at[my_slice, :], w.at[j, z, my_slice, :],
+                    s1_send.at[j], s1_recv.at[j, z], s, after,
+                )
+
     def exchange(g):
         for i in range(1, seq):
             to_s = lax.rem(s + i, seq)
@@ -72,12 +82,18 @@
     exchange(0)
     shard = width // head
     half = shard // 2
-    for i in range(1, head):
-        send(
-            wo.at[pl.ds(pl.multiple_of(parity * half, half), half), :],
-            w_o.at[pl.ds(pl.multiple_of(z * shard + parity * half, half), half), :],
-            o1_send, o1_recv.at[i - 1], s, lax.rem(z + i, head),
-        )
+    def out_rows(from_z):
+        return w_o.at[pl.ds(pl.multiple_of(from_z * shard + parity * half, half), half), :]
+
+    for _, _, after, open_ in ways(1):
+
+        @pl.when(open_)
+        def _():
+            send(
+                wo.at[pl.ds(pl.multiple_of(parity * half, half), half), :],
+                out_rows(z), o1_send, o1_recv.at[z], s, after,
+            )
+
     own = [pltpu.make_async_copy(weights[j], w.at[j, z], load_sem.at[j]) for j in range(3)]
     own.append(
         pltpu.make_async_copy(
@@ -91,17 +107,88 @@
     col = lax.broadcasted_iota(jnp.int32, (rows, rows), 1)
     bias[...] = jnp.where((row & (SUB - 1)) == (col & (SUB - 1)), 0.0, MASKED)
 
-    for j in range(3):
+    tall = max(n for n in range(1, half_seq + 1) if half_seq % n == 0 and n * n <= half_seq)
+    wide = half_seq // tall
+    up, across = place // wide, lax.rem(place, wide)
+
+    def device_at(a, b):
+        return (lax.rem(a, tall) * wide + lax.rem(b, wide)) * 2 + parity
+
+    def rows_at(a, b, start, size):
+        first = parity * half_seq + lax.rem(a, tall) * wide + lax.rem(b, wide)
+        return pl.ds(pl.multiple_of(first * slice_rows + start, size), size)
+
+    def spread(j):
+        for d in range(1, head):
+            for from_z, valid, after, open_ in ways(d):
+                piece = w.at[j, jnp.clip(from_z, 0, head - 1), my_slice, :]
+                arrived = s1_recv.at[j, jnp.clip(from_z, 0, head - 1)]
+
+                @pl.when(valid)
+                def _():
+                    drain(piece, arrived)
+
+                    @pl.when(open_)
+                    def _():
+                        send(piece, piece, s1_send.at[j], arrived, s, after)
+
+                    for k in range(1, wide):
+                        to_s = device_at(up, across + k)
+                        send(piece, piece, s2_send.at[j], s2_recv.at[j, k - 1], to_s, z)
+                    for k in range(1, tall):
+                        to_s = device_at(up + k, across)
+                        send(piece, piece, s2_send.at[j], s2_recv.at[j, wide + k - 2], to_s, z)
+
+    half_rows = slice_rows // 2
+
+    def relay(j):
+        for k in range(1, wide):
+            drain(w.at[j, pl.ds(0, head - 1), pl.ds(0, slice_rows), :], s2_recv.at[j, k - 1])
+            for i in range(1, head):
+                piece = w.at[
+                    j, lax.rem(z + i, head), rows_at(up, across + wide - k, 0, half_rows), :
+                ]
+                for n in range(1, tall):
+                    to_s = device_at(up + n, across)
+                    send(piece, piece, s2_send.at[j], far_recv.at[j], to_s, z)
+        for k in range(1, tall):
+            drain(
+                w.at[j, pl.ds(0, head - 1), pl.ds(0, slice_rows), :], s2_recv.at[j, wide + k - 2]
+            )
+            for i in range(1, head):
+                piece = w.at[
+                    j, lax.rem(z + i, head), rows_at(up + tall - k, across, half_rows, half_rows), :
+                ]
+                for n in range(1, wide):
+                    to_s = device_at(up, across + n)
+                    send(piece, piece, s2_send.at[j], far_recv.at[j], to_s, z)
+
+    far = (tall - 1) * (wide - 1) * slice_rows
+    parity_rows = pl.ds(
+        pl.multiple_of(parity * half_seq * slice_rows, slice_rows), half_seq * slice_rows
+    )
+
+    def to_sibling(j):
+        if far:
+            drain(w.at[j, pl.ds(0, head - 1), pl.ds(0, far), :], far_recv.at[j])
         for i in range(1, head):
-            from_z = lax.rem(z + head - i, head)
-            piece = w.at[j, from_z, my_slice, :]
-            drain(piece, s1_recv.at[j, i - 1])
-            for k in range(1, half_seq):
-                to_s = lax.rem(place + k, half_seq) * 2 + parity
-                send(piece, piece, s2_send.at[j], s2_recv.at[j], to_s, z)
-
-    for g in range(1, groups):
-        exchange(g)
+            piece = w.at[j, lax.rem(z + i, head), parity_rows, :]
+            send(piece, piece, s3_send.at[j], s3_recv.at[j], sibling, z)
+
+    def spread_out(d):
+        for from_z, valid, after, open_ in ways(d):
+            piece = out_rows(jnp.clip(from_z, 0, head - 1))
+            arrived = o1_recv.at[jnp.clip(from_z, 0, head - 1)]
+
+            @pl.when(valid)
+            def _():
+                drain(piece, arrived)
+
+                @pl.when(open_)
+                def _():
+                    send(piece, piece, o1_send, arrived, s, after)
+
+                send(piece, piece, o2_send, o2_recv, sibling, z)
 
     step_frames = 8
 
@@ -120,8 +207,6 @@
                 centered * lax.rsqrt(var + EPSILON)
             ).astype(jnp.bfloat16)
 
-    norm(0)
-
     def project(j):
         @pl.loop(0, head)
         def _(h):
@@ -131,28 +216,31 @@
             start = pl.multiple_of(h * columns, columns)
             qkv[j, :, pl.ds(start, columns)] = r.astype(jnp.bfloat16)
 
-    parity_rows = pl.ds(
-        pl.multiple_of(parity * half_seq * slice_rows, slice_rows), half_seq * slice_rows
-    )
-    for j in range(3):
+    def take(j):
         own[j].wait()
-        drain(
-            w.at[j, pl.ds(0, head - 1), pl.ds(0, (half_seq - 1) * slice_rows), :], s2_recv.at[j]
-        )
-        for i in range(1, head):
-            piece = w.at[j, lax.rem(z + i, head), parity_rows, :]
-            send(piece, piece, s3_send.at[j], s3_recv.at[j], sibling, z)
-        if j == 1:
-            for i in range(1, head):
-                from_z = lax.rem(z + head - i, head)
-                piece = w_o.at[
-                    pl.ds(pl.multiple_of(from_z * shard + parity * half, half), half), :
-                ]
-                drain(piece, o1_recv.at[i - 1])
-                send(piece, piece, o2_send, o2_recv, sibling, z)
         drain(w.at[j, pl.ds(0, head - 1), pl.ds(0, half_seq * slice_rows), :], s3_recv.at[j])
         project(j)
 
+    spread(0)
+    spread(1)
+    relay(0)
+    spread(2)
+    norm(0)
+    spread_out(1)
+    relay(1)
+    to_sibling(0)
+    for d in range(2, head - 1):
+        spread_out(d)
+    relay(2)
+    for g in range(1, groups):
+        exchange(g)
+    to_sibling(1)
+    take(0)
+    if head > 2:
+        spread_out(head - 1)
+    take(1)
+    to_sibling(2)
+    take(2)
     own[3].wait()
     drain(w_o.at[pl.ds(0, (head - 1) * half), :], o2_recv)
 
@@ -221,12 +309,24 @@
         drain(mixed.at[g, pl.ds(0, blocks - blocks // total)], out_send.at[g])
         drain(x.at[g, pl.ds(0, frames - own_frames)], tok_send.at[g])
     for j in range(3):
-        drain(w.at[j, pl.ds(0, head - 1), pl.ds(0, slice_rows), :], s1_send.at[j])
+        for d in range(head):
+            for from_z, valid, _, open_ in ways(d):
+
+                @pl.when(valid & open_)
+                def _():
+                    drain(w.at[j, 0, pl.ds(0, slice_rows), :], s1_send.at[j])
+
         drain(
             w.at[j, pl.ds(0, head - 1), pl.ds(0, (half_seq - 1) * slice_rows), :], s2_send.at[j]
         )
         drain(w.at[j, pl.ds(0, head - 1), pl.ds(0, half_seq * slice_rows), :], s3_send.at[j])
-    drain(w_o.at[pl.ds(0, (head - 1) * half), :], o1_send)
+    for d in range(head):
+        for from_z, valid, _, open_ in ways(d):
+
+            @pl.when(valid & open_)
+            def _():
+                drain(w_o.at[pl.ds(0, half), :], o1_send)
+
     drain(w_o.at[pl.ds(0, (head - 1) * half), :], o2_send)
 
 
@@ -254,8 +354,8 @@
             pltpu.VMEM((groups, head * frames, SUB, width // head), bf16),
             pltpu.VMEM((rows, rows), jnp.float32),
             dma((groups,)), dma((groups,)), dma((4,)),
-            dma((3,)), dma((3, head - 1)), dma((3,)), dma((3,)), dma((3,)), dma((3,)),
-            dma, dma((head - 1,)), dma, dma, dma((groups,)), dma,
+            dma((3,)), dma((3, head)), dma((3,)), dma((3, seq // 2)), dma((3,)), dma((3,)), dma((3,)),
+            dma, dma((head,)), dma, dma, dma((groups,)), dma,
         ],
         compiler_params=pltpu.CompilerParams(
             has_side_effects=True, vmem_limit_bytes=60 * 1024 * 1024

time: 106 us -> 102 us (0.962)
  Pallas kernels: 103 us -> 98.8 us
    pallas_call x1, Pallas kernels: 103 us -> 98.8 us  [local(): pl.pallas_call(functools.partial(kernel, seq, head), out_shape=jax.ShapeD...]
where the time goes in v4:
time: 102 us
  Pallas kernels  98.8 us (97%)
  local copies, waits for them, and re-layouts  3.05 us (3%)
    pallas_call x1, Pallas kernels, local(): pl.pallas_call(functools.partial(kernel, seq, head), out_shape=jax.ShapeD...  98.8 us
    unnamed x1, local copies, waits for them, and re-layouts  3.05 us

profile of v4, /device:TPU:0, one launch (start us, length us, event | category | flops | bytes accessed | tf_op | source)
XLA Modules:
  0.0 101.8 jit_solution(5545899878294461223)
XLA Ops:
  0.0 98.8 %shard_map.55 = bf16[4,1024,256]{2,1,0:T(8,128)(2,1)} custom-call(bf16[4,1024,1024]{2,1,0:T(8,128)(2,1)} %tok.1, bf16[1024,256]{1,0:T(8,128)(2,1)} %wq.1, bf16[1024,256]{1,0:T(8,128)(2,1)} %wk.1, bf16[1024,256]{1,0:T(8,128)(2,1)} %wv.1, bf16[256,1024]{1,0:T(8,128)(2,1)} %wo.1), custom_call_target="tpu_custom_call" | custom-call | tf_op jit(solution)/shard_map/pallas_call | solution.py:342
  98.8 3.0 %copy.7 = bf16[4,1024,256]{2,1,0:T(8,128)(2,1)} copy(bf16[4,1024,256]{2,1,0:T(8,128)(2,1)} %shard_map.55) | data formatting | bytes 4194304

commit v5 on v4

--- a/solution.py
+++ b/solution.py
@@ -208,7 +208,7 @@
             ).astype(jnp.bfloat16)
 
     def project(j):
-        @pl.loop(0, head)
+        @pl.loop(0, head, unroll=True)
         def _(h):
             r = jnp.dot(normed[...], w[j, h], preferred_element_type=jnp.float32)
             if j == 0:
@@ -236,14 +236,11 @@
         exchange(g)
     to_sibling(1)
     take(0)
-    if head > 2:
-        spread_out(head - 1)
     take(1)
     to_sibling(2)
     take(2)
-    own[3].wait()
-    drain(w_o.at[pl.ds(0, (head - 1) * half), :], o2_recv)
-
+    if head > 2:
+        spread_out(head - 1)
     pair = 2 * HS
     left = lax.broadcasted_iota(jnp.int32, (rows, pair), 1) < HS
     left_b = left.astype(jnp.float32).astype(jnp.bfloat16)
@@ -255,8 +252,8 @@
         start = pl.multiple_of(z * quarter + s * own_patches + g * SUB, SUB)
         return out.at[:, pl.ds(start, SUB), :]
 
-    def finish(g):
-        @pl.loop(0, width // pair)
+    def finish(g, first=False):
+        @pl.loop(0, width // pair, unroll=4)
         def _(n):
             lanes = pl.ds(pl.multiple_of(n * pair, pair), pair)
             q, k, v = qkv[0, :, lanes], qkv[1, :, lanes], qkv[2, :, lanes]
@@ -273,7 +270,11 @@
                 results.append(r[:, :pair] / r[:, pair:])
             att[:, lanes] = jnp.where(left, results[0], results[1]).astype(jnp.bfloat16)
 
-        @pl.loop(0, head)
+        if first:
+            own[3].wait()
+            drain(w_o.at[pl.ds(0, (head - 1) * half), :], o2_recv)
+
+        @pl.loop(0, head, unroll=True)
         def _(h):
             lanes = pl.ds(pl.multiple_of(h * columns, columns), columns)
             r = jnp.dot(att[...], w_o[:, lanes], preferred_element_type=jnp.float32)
@@ -294,7 +295,7 @@
             mixed.at[g, pl.ds(z * frames + s * own_frames, own_frames)], out_block(g), out_recv
         ).start()
 
-    finish(0)
+    finish(0, True)
 
     @pl.loop(1, groups)
     def _(g):

time: 102 us -> 98.8 us (0.969)
  Pallas kernels: 98.8 us -> 95.6 us
    pallas_call x1, Pallas kernels: 98.8 us -> 95.6 us  [local(): pl.pallas_call(functools.partial(kernel, seq, head), out_shape=jax.ShapeD...]
where the time goes in v5:
time: 98.8 us; the launch traced here: 98.6 us
  Pallas kernels  95.6 us (97%)
  local copies, waits for them, and re-layouts  3.05 us (3%)
    pallas_call x1, Pallas kernels, local(): pl.pallas_call(functools.partial(kernel, seq, head), out_shape=jax.ShapeD...  95.6 us
    unnamed x1, local copies, waits for them, and re-layouts  3.05 us

profile of v5, /device:TPU:0, one launch (start us, length us, event | category | flops | bytes accessed | tf_op | source)
XLA Modules:
  0.0 98.6 jit_solution(17279215353999768968)
XLA Ops:
  0.0 95.6 %shard_map.55 = bf16[4,1024,256]{2,1,0:T(8,128)(2,1)} custom-call(bf16[4,1024,1024]{2,1,0:T(8,128)(2,1)} %tok.1, bf16[1024,256]{1,0:T(8,128)(2,1)} %wq.1, bf16[1024,256]{1,0:T(8,128)(2,1)} %wk.1, bf16[1024,256]{1,0:T(8,128)(2,1)} %wv.1, bf16[256,1024]{1,0:T(8,128)(2,1)} %wo.1), custom_call_target="tpu_custom_call" | custom-call | tf_op jit(solution)/shard_map/pallas_call | solution.py:343
  95.6 3.0 %copy.7 = bf16[4,1024,256]{2,1,0:T(8,128)(2,1)} copy(bf16[4,1024,256]{2,1,0:T(8,128)(2,1)} %shard_map.55) | data formatting | bytes 4194304
